TPU v7x, 32 devices: a whole 2x2x4 slice. The times are simulated.
32 devices in a mesh: tm: 2 (over x), lat: 4 (over y, core), lon: 4 (over z).
Axes of the slice: x: 2, y: 2, z: 4, core: 2. Of those that a mesh axis runs over, the one named last changes fastest.
Arguments:
- forcing: float32 [8, 512, 2048], P('tm', 'lat', 'lon'), may hold values from -17 to 17
- depth: float32 [512, 2048], P('lat', 'lon'), may hold values from 0.2 to 2
- mask: int32 [512, 2048], P('lat', 'lon'), may hold values 0 or 1
- guess: float32 [2, 512, 2048], P('tm', 'lat', 'lon'), may hold values from -6 to 6
Outputs:
- adjoint: float32 [8, 512, 2048], P('tm', 'lat', 'lon')
All inputs are finite; a program needn't handle non-finite values. No bound on the sum of `mask` on one device may be relied on, other than what follows from the above.
Results may differ from a plain program's by a relative error of at most 0.0001.
Values sent between devices are 32-bit elements; how exact they have to be, the bound alone decides.
No kernel may reach another device: no remote copies, remote signals or barrier semaphores. Data moves between devices by JAX's collectives and lax.ppermute only.
A program may use at most 64 MiB of HBM per device.

v0:
```python
import jax
import jax.numpy as jnp
from jax import lax
from jax.sharding import PartitionSpec as P

FS = 4
FINE_ITERS = 2
COUPLING = 3.0
EPSILON = 1e-06


def with_halo(block, sides, width):
    for axis, dim in sides:
        count = lax.axis_size(axis)
        forward = [(i, i + 1) for i in range(count - 1)]
        forward.append((count - 1, 0))
        backward = [(target, source) for source, target in forward]
        low = lax.ppermute(
            lax.slice_in_dim(block, block.shape[dim] - width, None, axis=dim), axis, forward
        )
        high = lax.ppermute(lax.slice_in_dim(block, 0, width, axis=dim), axis, backward)
        block = jnp.concatenate([low, block, high], axis=dim)
    return block


def shifted(array, axis, by):
    size = lax.axis_size(axis)
    pairs = [(i, i + by) for i in range(size) if 0 <= i + by < size]
    return lax.ppermute(array, axis, pairs)


def face_terms(depth, mask):
    wet = mask.astype(jnp.float32)
    stacked = jnp.stack([wet, depth])
    padded = with_halo(stacked, (("lat", 1), ("lon", 2)), 1)
    rows = depth.shape[0]
    wet_pad = padded[0]
    deep_pad = padded[1]
    middle_wet = wet_pad[1:-1]
    middle_deep = deep_pad[1:-1]
    across = (
        COUPLING
        * middle_wet[:, :-1]
        * middle_wet[:, 1:]
        * 0.5
        * (middle_deep[:, :-1] + middle_deep[:, 1:])
    )
    along = (
        COUPLING
        * wet_pad[:-1, 1:-1]
        * wet_pad[1:, 1:-1]
        * 0.5
        * (deep_pad[:-1, 1:-1] + deep_pad[1:, 1:-1])
    )
    first = lax.axis_index("lat") == 0
    final = lax.axis_index("lat") == lax.axis_size("lat") - 1
    face_row = lax.broadcasted_iota(jnp.int32, along.shape, 0)
    along = jnp.where(first & (face_row == 0) | final & (face_row == rows), 0.0, along)
    return (across[:, 1:], across[:, :-1], along[1:], along[:-1])


def apply_op(field, faces, factor):
    east, west, north, south = faces
    padded = with_halo(field, (("lat", 0), ("lon", 1)), 1)
    spread = east * (field - padded[1:-1, 2:]) + west * (field - padded[1:-1, :-2])
    spread = spread + north * (field - padded[2:, 1:-1]) + south * (field - padded[:-2, 1:-1])
    return field + factor * spread


def paired(residual, image):
    return lax.psum((jnp.sum(residual * residual), jnp.sum(residual * image)), ("lat", "lon"))


def fine_solve(source, faces):
    solution = jnp.zeros_like(source)
    residual = source
    direction = source
    image = apply_op(source, faces, 1.0)
    norm_now, product = paired(source, image)
    alpha = norm_now / (product + EPSILON)
    along = image
    for level in range(FINE_ITERS):
        solution = solution + alpha * direction
        residual = residual - alpha * along
        if level + 1 < FINE_ITERS:
            image = apply_op(residual, faces, 1.0)
            norm_next, product = paired(residual, image)
            ratio = norm_next / (norm_now + EPSILON)
            alpha = norm_next / (product - ratio * norm_next / alpha + EPSILON)
            direction = residual + ratio * direction
            along = image + ratio * along
            norm_now = norm_next
    return solution


def coarse_solve(source, faces):
    image = apply_op(source, faces, float(FS))
    norm_now, product = lax.psum(
        (jnp.sum(source * source), jnp.sum(source * image)), ("lat", "lon")
    )
    return norm_now / (product + EPSILON) * source


def local(forcing, depth, mask, guess):
    faces = face_terms(depth, mask)
    start = guess[0]
    value = start
    for level in range(FS - 1, 0, -1):
        value = fine_solve(value, faces) + forcing[level]
    finished = fine_solve(value, faces) + forcing[0]
    offset = finished - coarse_solve(start, faces)
    position = lax.axis_index("tm")
    slab_count = lax.axis_size("tm")
    is_final = position == slab_count - 1

    def turn(index, upper):
        here = coarse_solve(upper, faces) + offset
        moved = shifted(here, "tm", -1)
        return jnp.where(is_final, start, moved)

    upper = lax.fori_loop(0, slab_count - 1, turn, start)
    here = coarse_solve(upper, faces) + offset
    value = upper
    later = []
    for level in range(FS - 1, 0, -1):
        value = fine_solve(value, faces) + forcing[level]
        later.append(value)
    return jnp.stack([here] + later[::-1])


def solution(mesh):
    return jax.shard_map(
        local,
        mesh=mesh,
        in_specs=(P("tm", "lat", "lon"), P("lat", "lon"), P("lat", "lon"), P("tm", "lat", "lon")),
        out_specs=P("tm", "lat", "lon"),
        check_vma=False,
    )
```

profile of v0, /device:TPU:0, one launch (start us, length us, event | category | flops | bytes accessed | tf_op | source)
XLA Modules:
  0.0 654.5 jit_solution(5138492691054062486)
XLA Ops:
  13.9 3.4 collective-permute-done.3
  20.8 31.9 %all-reduce.13 = (f32[]{:T(128)}, f32[]{:T(128)}) all-reduce(f32[]{:T(128)} %get-tuple-element.47, f32[]{:T(128)} %get-tuple-element.22), channel_id=1, replica_groups=mesh['tm'=2,'lat'=4,'lon'=4] {'lat','lon'}, use_global_device_ids=true, to_apply=%region_1.2 | all-reduce | flops 2 | bytes 16 | tf_op jit(solution)/shard_map/while/body/eval_jaxpr/psum | solution.py:98
  64.6 31.9 %all-reduce.12 = (f32[]{:T(128)}, f32[]{:T(128)}) all-reduce(f32[]{:T(128)} %get-tuple-element.61, f32[]{:T(128)} %get-tuple-element.60), channel_id=1, replica_groups=mesh['tm'=2,'lat'=4,'lon'=4] {'lat','lon'}, use_global_device_ids=true, to_apply=%region_7.8 | all-reduce | flops 2 | bytes 16 | tf_op jit(solution)/shard_map/psum | solution.py:71
  105.2 2.7 collective-permute-done.14
  110.5 32.1 %all-reduce.11 = (f32[]{:T(128)}, f32[]{:T(128)}) all-reduce(f32[]{:T(128)} %get-tuple-element.59, f32[]{:T(128)} %get-tuple-element.58), channel_id=1, replica_groups=mesh['tm'=2,'lat'=4,'lon'=4] {'lat','lon'}, use_global_device_ids=true, to_apply=%region_11.12 | all-reduce | flops 2 | bytes 16 | tf_op jit(solution)/shard_map/psum | solution.py:71
  154.9 31.1 %all-reduce.10 = (f32[]{:T(128)}, f32[]{:T(128)}) all-reduce(f32[]{:T(128)} %get-tuple-element.57, f32[]{:T(128)} %get-tuple-element.56), channel_id=1, replica_groups=mesh['tm'=2,'lat'=4,'lon'=4] {'lat','lon'}, use_global_device_ids=true, to_apply=%region_15.16 | all-reduce | flops 2 | bytes 16 | tf_op jit(solution)/shard_map/psum | solution.py:71
  194.4 2.7 collective-permute-done.22
  197.1 2.8 collective-permute-done.23
  200.9 32.0 %all-reduce.9 = (f32[]{:T(128)}, f32[]{:T(128)}) all-reduce(f32[]{:T(128)} %get-tuple-element.55, f32[]{:T(128)} %get-tuple-element.54), channel_id=1, replica_groups=mesh['tm'=2,'lat'=4,'lon'=4] {'lat','lon'}, use_global_device_ids=true, to_apply=%region_19.20 | all-reduce | flops 2 | bytes 16 | tf_op jit(solution)/shard_map/psum | solution.py:71
  245.3 31.3 %all-reduce.8 = (f32[]{:T(128)}, f32[]{:T(128)}) all-reduce(f32[]{:T(128)} %get-tuple-element.53, f32[]{:T(128)} %get-tuple-element.52), channel_id=1, replica_groups=mesh['tm'=2,'lat'=4,'lon'=4] {'lat','lon'}, use_global_device_ids=true, to_apply=%region_23.24 | all-reduce | flops 2 | bytes 16 | tf_op jit(solution)/shard_map/psum | solution.py:71
  291.1 31.6 %all-reduce.7 = (f32[]{:T(128)}, f32[]{:T(128)}) all-reduce(f32[]{:T(128)} %get-tuple-element.51, f32[]{:T(128)} %get-tuple-element.50), channel_id=1, replica_groups=mesh['tm'=2,'lat'=4,'lon'=4] {'lat','lon'}, use_global_device_ids=true, to_apply=%region_27.28 | all-reduce | flops 2 | bytes 16 | tf_op jit(solution)/shard_map/psum | solution.py:71
  334.8 32.4 %all-reduce.6 = (f32[]{:T(128)}, f32[]{:T(128)}, f32[]{:T(128)}) all-reduce(f32[]{:T(128)} %get-tuple-element.49, f32[]{:T(128)} %get-tuple-element.48, f32[]{:T(128)} %get-tuple-element.21), channel_id=1, replica_groups=mesh['tm'=2,'lat'=4,'lon'=4] {'lat','lon'}, use_global_device_ids=true, to_apply=%region_31.32 | all-reduce | flops 3 | bytes 24 | tf_op jit(solution)/shard_map/psum | solution.py:71
  373.1 7.0 %collective-permute-done.36 = f32[128,512]{1,0:T(8,128)S(1)} collective-permute-done((f32[128,512]{1,0:T(8,128)S(1)}, f32[128,512]{1,0:T(8,128)S(1)}, u32[]{:S(2)}, u32[]{:S(2)}) %collective-permute-start.36) | collective-permute-done | bytes 262176 | tf_op jit(solution)/shard_map/while/body/eval_jaxpr/ppermute | solution.py:29
  385.4 2.9 collective-permute-done.39
  388.3 3.0 collective-permute-done.40
  392.2 30.8 %all-reduce.5 = (f32[]{:T(128)}, f32[]{:T(128)}) all-reduce(f32[]{:T(128)} %get-tuple-element.25, f32[]{:T(128)} %get-tuple-element.24), channel_id=1, replica_groups=mesh['tm'=2,'lat'=4,'lon'=4] {'lat','lon'}, use_global_device_ids=true, to_apply=%region_35.36 | all-reduce | flops 2 | bytes 16 | tf_op jit(solution)/shard_map/psum | solution.py:98
  432.3 3.2 collective-permute-done.44
  436.4 32.0 %all-reduce.4 = (f32[]{:T(128)}, f32[]{:T(128)}) all-reduce(f32[]{:T(128)} %get-tuple-element.46, f32[]{:T(128)} %get-tuple-element.45), channel_id=1, replica_groups=mesh['tm'=2,'lat'=4,'lon'=4] {'lat','lon'}, use_global_device_ids=true, to_apply=%region_41.42 | all-reduce | flops 2 | bytes 16 | tf_op jit(solution)/shard_map/psum | solution.py:71
  477.3 3.0 collective-permute-done.47
  483.1 31.3 %all-reduce.3 = (f32[]{:T(128)}, f32[]{:T(128)}) all-reduce(f32[]{:T(128)} %get-tuple-element.44, f32[]{:T(128)} %get-tuple-element.43), channel_id=1, replica_groups=mesh['tm'=2,'lat'=4,'lon'=4] {'lat','lon'}, use_global_device_ids=true, to_apply=%region_45.46 | all-reduce | flops 2 | bytes 16 | tf_op jit(solution)/shard_map/psum | solution.py:71
  527.1 31.3 %all-reduce.2 = (f32[]{:T(128)}, f32[]{:T(128)}) all-reduce(f32[]{:T(128)} %get-tuple-element.42, f32[]{:T(128)} %get-tuple-element.41), channel_id=1, replica_groups=mesh['tm'=2,'lat'=4,'lon'=4] {'lat','lon'}, use_global_device_ids=true, to_apply=%region_49.50 | all-reduce | flops 2 | bytes 16 | tf_op jit(solution)/shard_map/psum | solution.py:71
  567.0 2.8 collective-permute-done.55
  573.2 31.8 %all-reduce.1 = (f32[]{:T(128)}, f32[]{:T(128)}) all-reduce(f32[]{:T(128)} %get-tuple-element.40, f32[]{:T(128)} %get-tuple-element.38), channel_id=1, replica_groups=mesh['tm'=2,'lat'=4,'lon'=4] {'lat','lon'}, use_global_device_ids=true, to_apply=%region_53.54 | all-reduce | flops 2 | bytes 16 | tf_op jit(solution)/shard_map/psum | solution.py:71
  617.0 31.8 %all-reduce = (f32[]{:T(128)}, f32[]{:T(128)}, f32[]{:T(128)}) all-reduce(f32[]{:T(128)} %get-tuple-element.36, f32[]{:T(128)} %get-tuple-element.26, f32[]{:T(128)} %get-tuple-element.23), channel_id=1, replica_groups=mesh['tm'=2,'lat'=4,'lon'=4] {'lat','lon'}, use_global_device_ids=true, to_apply=%region_57.58 | all-reduce | flops 3 | bytes 24 | tf_op jit(solution)/shard_map/psum | solution.py:71
  (185 shorter events, 139.5 us)
Async XLA Ops:
  3.6 6.4 collective-permute-start.4
  4.3 5.7 collective-permute-start.5
  5.6 8.4 %collective-permute-start.2 = (f32[2,130,1]{2,1,0:T(8,128)S(1)}, f32[2,130,1]{2,1,0:T(8,128)S(1)}, u32[]{:S(2)}, u32[]{:S(2)}) collective-permute-start(f32[2,130,1]{2,1,0:T(8,128)S(1)} %get-tuple-element.105), channel_id=1, source_target_pairs={{0,1},{1,2},{2,3},{3,0},{4,5},{5,6},{6,7},{7,4},{8,9},{9,10},{10,1... | collective-permute-start | bytes 3128 | tf_op jit(solution)/shard_map/ppermute | solution.py:18
  7.9 9.4 %collective-permute-start.3 = (f32[2,130,1]{2,1,0:T(8,128)S(1)}, f32[2,130,1]{2,1,0:T(8,128)S(1)}, u32[]{:S(2)}, u32[]{:S(2)}) collective-permute-start(f32[2,130,1]{2,1,0:T(8,128)S(1)} %get-tuple-element.106), channel_id=1, source_target_pairs={{1,0},{2,1},{3,2},{0,3},{5,4},{6,5},{7,6},{4,7},{9,8},{10,9},{11,1... | collective-permute-start | bytes 3128 | tf_op jit(solution)/shard_map/ppermute | solution.py:21
  10.1 9.2 %collective-permute-start.6 = (f32[130,1]{1,0:T(8,128)S(1)}, f32[130,1]{1,0:T(8,128)S(1)}, u32[]{:S(2)}, u32[]{:S(2)}) collective-permute-start(f32[130,1]{1,0:T(8,128)S(1)} %get-tuple-element.135), channel_id=1, source_target_pairs={{1,0},{2,1},{3,2},{0,3},{5,4},{6,5},{7,6},{4,7},{9,8},{10,9},{11,1... | collective-permute-start | bytes 1568 | tf_op jit(solution)/shard_map/while/body/eval_jaxpr/ppermute | solution.py:21
  12.1 7.7 %collective-permute-start.7 = (f32[130,1]{1,0:T(8,128)S(1)}, f32[130,1]{1,0:T(8,128)S(1)}, u32[]{:S(2)}, u32[]{:S(2)}) collective-permute-start(f32[130,1]{1,0:T(8,128)S(1)} %get-tuple-element.136), channel_id=1, source_target_pairs={{0,1},{1,2},{2,3},{3,0},{4,5},{5,6},{6,7},{7,4},{8,9},{9,10},{10,1... | collective-permute-start | bytes 1568 | tf_op jit(solution)/shard_map/while/body/eval_jaxpr/ppermute | solution.py:18
  57.4 6.3 collective-permute-start.11
  103.1 6.4 collective-permute-start.15
  147.0 5.1 collective-permute-start.18
  147.0 6.9 %collective-permute-start.19 = (f32[130,1]{1,0:T(8,128)S(1)}, f32[130,1]{1,0:T(8,128)S(1)}, u32[]{:S(2)}, u32[]{:S(2)}) collective-permute-start(f32[130,1]{1,0:T(8,128)S(1)} %get-tuple-element.130), channel_id=1, source_target_pairs={{0,1},{1,2},{2,3},{3,0},{4,5},{5,6},{6,7},{7,4},{8,9},{9,10},{10,1... | collective-permute-start | bytes 1568 | tf_op jit(solution)/shard_map/ppermute | solution.py:18
  193.0 7.0 %collective-permute-start.23 = (f32[130,1]{1,0:T(8,128)S(1)}, f32[130,1]{1,0:T(8,128)S(1)}, u32[]{:S(2)}, u32[]{:S(2)}) collective-permute-start(f32[130,1]{1,0:T(8,128)S(1)} %get-tuple-element.128), channel_id=1, source_target_pairs={{0,1},{1,2},{2,3},{3,0},{4,5},{5,6},{6,7},{7,4},{8,9},{9,10},{10,1... | collective-permute-start | bytes 1568 | tf_op jit(solution)/shard_map/ppermute | solution.py:18
  237.3 5.1 collective-permute-start.26
  237.4 6.9 %collective-permute-start.27 = (f32[130,1]{1,0:T(8,128)S(1)}, f32[130,1]{1,0:T(8,128)S(1)}, u32[]{:S(2)}, u32[]{:S(2)}) collective-permute-start(f32[130,1]{1,0:T(8,128)S(1)} %get-tuple-element.126), channel_id=1, source_target_pairs={{0,1},{1,2},{2,3},{3,0},{4,5},{5,6},{6,7},{7,4},{8,9},{9,10},{10,1... | collective-permute-start | bytes 1568 | tf_op jit(solution)/shard_map/ppermute | solution.py:18
  283.4 6.7 %collective-permute-start.31 = (f32[130,1]{1,0:T(8,128)S(1)}, f32[130,1]{1,0:T(8,128)S(1)}, u32[]{:S(2)}, u32[]{:S(2)}) collective-permute-start(f32[130,1]{1,0:T(8,128)S(1)} %get-tuple-element.124), channel_id=1, source_target_pairs={{0,1},{1,2},{2,3},{3,0},{4,5},{5,6},{6,7},{7,4},{8,9},{9,10},{10,1... | collective-permute-start | bytes 1568 | tf_op jit(solution)/shard_map/ppermute | solution.py:18
  327.2 6.6 %collective-permute-start.35 = (f32[130,1]{1,0:T(8,128)S(1)}, f32[130,1]{1,0:T(8,128)S(1)}, u32[]{:S(2)}, u32[]{:S(2)}) collective-permute-start(f32[130,1]{1,0:T(8,128)S(1)} %get-tuple-element.122), channel_id=1, source_target_pairs={{0,1},{1,2},{2,3},{3,0},{4,5},{5,6},{6,7},{7,4},{8,9},{9,10},{10,1... | collective-permute-start | bytes 1568 | tf_op jit(solution)/shard_map/ppermute | solution.py:18
  371.8 8.3 %collective-permute-start.36 = (f32[128,512]{1,0:T(8,128)S(1)}, f32[128,512]{1,0:T(8,128)S(1)}, u32[]{:S(2)}, u32[]{:S(2)}) collective-permute-start(f32[128,512]{1,0:T(8,128)S(1)} %get-tuple-element.95), channel_id=1, source_target_pairs={{16,0},{17,1},{18,2},{19,3},{20,4},{21,5},{22,6},{23,7},{24,8},{25... | collective-permute-start | bytes 786440 | tf_op jit(solution)/shard_map/while/body/eval_jaxpr/ppermute | solution.py:29
  383.3 5.0 collective-permute-start.39
  384.8 6.5 collective-permute-start.40
  428.6 6.9 %collective-permute-start.44 = (f32[130,1]{1,0:T(8,128)S(1)}, f32[130,1]{1,0:T(8,128)S(1)}, u32[]{:S(2)}, u32[]{:S(2)}) collective-permute-start(f32[130,1]{1,0:T(8,128)S(1)} %get-tuple-element.118), channel_id=1, source_target_pairs={{0,1},{1,2},{2,3},{3,0},{4,5},{5,6},{6,7},{7,4},{8,9},{9,10},{10,1... | collective-permute-start | bytes 1568 | tf_op jit(solution)/shard_map/ppermute | solution.py:18
  475.2 5.1 collective-permute-start.47
  475.3 6.9 %collective-permute-start.48 = (f32[130,1]{1,0:T(8,128)S(1)}, f32[130,1]{1,0:T(8,128)S(1)}, u32[]{:S(2)}, u32[]{:S(2)}) collective-permute-start(f32[130,1]{1,0:T(8,128)S(1)} %get-tuple-element.116), channel_id=1, source_target_pairs={{0,1},{1,2},{2,3},{3,0},{4,5},{5,6},{6,7},{7,4},{8,9},{9,10},{10,1... | collective-permute-start | bytes 1568 | tf_op jit(solution)/shard_map/ppermute | solution.py:18
  519.3 6.8 %collective-permute-start.52 = (f32[130,1]{1,0:T(8,128)S(1)}, f32[130,1]{1,0:T(8,128)S(1)}, u32[]{:S(2)}, u32[]{:S(2)}) collective-permute-start(f32[130,1]{1,0:T(8,128)S(1)} %get-tuple-element.114), channel_id=1, source_target_pairs={{0,1},{1,2},{2,3},{3,0},{4,5},{5,6},{6,7},{7,4},{8,9},{9,10},{10,1... | collective-permute-start | bytes 1568 | tf_op jit(solution)/shard_map/ppermute | solution.py:18
  565.3 6.9 %collective-permute-start.56 = (f32[130,1]{1,0:T(8,128)S(1)}, f32[130,1]{1,0:T(8,128)S(1)}, u32[]{:S(2)}, u32[]{:S(2)}) collective-permute-start(f32[130,1]{1,0:T(8,128)S(1)} %get-tuple-element.112), channel_id=1, source_target_pairs={{0,1},{1,2},{2,3},{3,0},{4,5},{5,6},{6,7},{7,4},{8,9},{9,10},{10,1... | collective-permute-start | bytes 1568 | tf_op jit(solution)/shard_map/ppermute | solution.py:18
  609.4 6.7 %collective-permute-start.60 = (f32[130,1]{1,0:T(8,128)S(1)}, f32[130,1]{1,0:T(8,128)S(1)}, u32[]{:S(2)}, u32[]{:S(2)}) collective-permute-start(f32[130,1]{1,0:T(8,128)S(1)} %get-tuple-element.110), channel_id=1, source_target_pairs={{0,1},{1,2},{2,3},{3,0},{4,5},{5,6},{6,7},{7,4},{8,9},{9,10},{10,1... | collective-permute-start | bytes 1568 | tf_op jit(solution)/shard_map/ppermute | solution.py:18
  (40 other events, 179.6 us)
where the time goes:
time: 655 us
  blocking collectives  443 us (68%)
  waiting for transfers between devices  91.6 us (14%)
  starting transfers between devices  62.6 us (10%)
  between operations  38.4 us (6%)
  other arithmetic  18.7 us (3%)
    psum x12, blocking collectives, paired(): lax.psum((jnp.sum(residual * residual), jnp.sum(residual * image)), ('lat...  380 us
    psum x2, blocking collectives, coarse_solve(): lax.psum((jnp.sum(source * source), jnp.sum(source * image)), ('lat', 'lo...  62.6 us
    ppermute x30, waiting for transfers between devices, with_halo(): lax.ppermute(lax.slice_in_dim(block, block.shape[dim] - width, None, axis...  48.1 us
    ppermute x30, waiting for transfers between devices, with_halo(): lax.ppermute(lax.slice_in_dim(block, 0, width, axis=dim), axis, backward)  36.5 us
    ppermute x30, starting transfers between devices, with_halo(): lax.ppermute(lax.slice_in_dim(block, 0, width, axis=dim), axis, backward)  34.5 us
    ppermute x30, starting transfers between devices, with_halo(): lax.ppermute(lax.slice_in_dim(block, block.shape[dim] - width, None, axis...  26.8 us
  transfers between devices with their start and end apart: 61, of which 44 were waited for; matrix products, arithmetic and copies ran while one was open for 0% of the time, Pallas kernels for 0%

commit v1 on v0

--- a/solution.py
+++ b/solution.py
@@ -68,7 +68,9 @@
 
 
 def paired(residual, image):
-    return lax.psum((jnp.sum(residual * residual), jnp.sum(residual * image)), ("lat", "lon"))
+    return lax.psum(
+        lax.psum((jnp.sum(residual * residual), jnp.sum(residual * image)), "lon"), "lat"
+    )
 
 
 def fine_solve(source, faces):

time: 655 us -> 508 us (0.78)
  blocking collectives: 443 us -> 284 us
  waiting for transfers between devices: 91.6 us -> 120 us
  starting transfers between devices: 62.6 us -> 45.9 us
    psum x12 -> x28, blocking collectives: 380 us -> 220 us  [the longest x14 132 us: paired(): lax.psum((jnp.sum(residual * residual), jnp.sum(residual * image)), 'lon')]
    ppermute x30, waiting for transfers between devices: 48.1 us -> 66.5 us  [with_halo(): lax.ppermute(lax.slice_in_dim(block, block.shape[dim] - width, None, axis...]
    ppermute x30, starting transfers between devices: 26.8 us -> 8.93 us  [with_halo(): lax.ppermute(lax.slice_in_dim(block, block.shape[dim] - width, None, axis...]
    ppermute x30, waiting for transfers between devices: 36.5 us -> 44.4 us  [with_halo(): lax.ppermute(lax.slice_in_dim(block, 0, width, axis=dim), axis, backward)]
  transfers between devices with their start and end apart: 61 -> 61, of which waited for: 44 -> 57; matrix products, arithmetic and copies ran while one was open for 0% -> 0% of each run, Pallas kernels for 0% -> 0%
where the time goes in v1:
time: 508 us; the launch traced here: 507 us
  blocking collectives  284 us (56%)
  waiting for transfers between devices  120 us (24%)
  starting transfers between devices  45.9 us (9%)
  between operations  38.3 us (8%)
  other arithmetic  18.7 us (4%)
    psum x14, blocking collectives, paired(): lax.psum((jnp.sum(residual * residual), jnp.sum(residual * image)), 'lon')  132 us
    psum x14, blocking collectives, paired(): lax.psum(lax.psum((jnp.sum(residual * residual), jnp.sum(residual * image...  88.4 us
    ppermute x30, waiting for transfers between devices, with_halo(): lax.ppermute(lax.slice_in_dim(block, block.shape[dim] - width, None, axis...  66.5 us
    psum x2, blocking collectives, coarse_solve(): lax.psum((jnp.sum(source * source), jnp.sum(source * image)), ('lat', 'lo...  63.4 us
    ppermute x30, waiting for transfers between devices, with_halo(): lax.ppermute(lax.slice_in_dim(block, 0, width, axis=dim), axis, backward)  44.4 us
    ppermute x30, starting transfers between devices, with_halo(): lax.ppermute(lax.slice_in_dim(block, 0, width, axis=dim), axis, backward)  35.6 us
    reduce_sum x12, other arithmetic, paired(): jnp.sum(residual * image)  11.5 us
  transfers between devices with their start and end apart: 61, of which 57 were waited for; matrix products, arithmetic and copies ran while one was open for 0% of the time, Pallas kernels for 0%

profile of v1, /device:TPU:0, one launch (start us, length us, event | category | flops | bytes accessed | tf_op | source)
XLA Modules:
  0.0 507.0 jit_solution(1696705771883466837)
XLA Ops:
  22.7 10.9 %all-reduce.15 = (f32[]{:T(128)}, f32[]{:T(128)}) all-reduce(f32[]{:T(128)} %get-tuple-element.47, f32[]{:T(128)} %get-tuple-element.22), channel_id=1, replica_groups=mesh['tm'=2,'lat'=4,'lon'=4] {'lon'}, use_global_device_ids=true, to_apply=%region_4.5 | all-reduce | flops 2 | bytes 16 | tf_op jit(solution)/shard_map/psum | solution.py:72
  33.6 6.3 %all-reduce.29 = (f32[]{:T(128)}, f32[]{:T(128)}) all-reduce(f32[]{:T(128)} %get-tuple-element.92, f32[]{:T(128)} %get-tuple-element.93), channel_id=1, replica_groups=mesh['tm'=2,'lat'=4,'lon'=4] {'lat'}, use_global_device_ids=true, to_apply=%region_5.6 | all-reduce | flops 2 | bytes 16 | tf_op jit(solution)/shard_map/psum | solution.py:71
  52.1 9.9 %all-reduce.14 = (f32[]{:T(128)}, f32[]{:T(128)}) all-reduce(f32[]{:T(128)} %get-tuple-element.61, f32[]{:T(128)} %get-tuple-element.60), channel_id=1, replica_groups=mesh['tm'=2,'lat'=4,'lon'=4] {'lon'}, use_global_device_ids=true, to_apply=%region_10.11 | all-reduce | flops 2 | bytes 16 | tf_op jit(solution)/shard_map/psum | solution.py:72
  83.4 9.1 %all-reduce.13 = (f32[]{:T(128)}, f32[]{:T(128)}) all-reduce(f32[]{:T(128)} %get-tuple-element.59, f32[]{:T(128)} %get-tuple-element.58), channel_id=1, replica_groups=mesh['tm'=2,'lat'=4,'lon'=4] {'lon'}, use_global_device_ids=true, to_apply=%region_16.17 | all-reduce | flops 2 | bytes 16 | tf_op jit(solution)/shard_map/psum | solution.py:72
  92.4 6.3 %all-reduce.27 = (f32[]{:T(128)}, f32[]{:T(128)}) all-reduce(f32[]{:T(128)} %get-tuple-element.88, f32[]{:T(128)} %get-tuple-element.89), channel_id=1, replica_groups=mesh['tm'=2,'lat'=4,'lon'=4] {'lat'}, use_global_device_ids=true, to_apply=%region_17.18 | all-reduce | flops 2 | bytes 16 | tf_op jit(solution)/shard_map/psum | solution.py:71
  112.7 9.1 %all-reduce.12 = (f32[]{:T(128)}, f32[]{:T(128)}) all-reduce(f32[]{:T(128)} %get-tuple-element.57, f32[]{:T(128)} %get-tuple-element.56), channel_id=1, replica_groups=mesh['tm'=2,'lat'=4,'lon'=4] {'lon'}, use_global_device_ids=true, to_apply=%region_22.23 | all-reduce | flops 2 | bytes 16 | tf_op jit(solution)/shard_map/psum | solution.py:72
  144.0 9.1 %all-reduce.11 = (f32[]{:T(128)}, f32[]{:T(128)}) all-reduce(f32[]{:T(128)} %get-tuple-element.55, f32[]{:T(128)} %get-tuple-element.54), channel_id=1, replica_groups=mesh['tm'=2,'lat'=4,'lon'=4] {'lon'}, use_global_device_ids=true, to_apply=%region_28.29 | all-reduce | flops 2 | bytes 16 | tf_op jit(solution)/shard_map/psum | solution.py:72
  153.0 6.3 %all-reduce.25 = (f32[]{:T(128)}, f32[]{:T(128)}) all-reduce(f32[]{:T(128)} %get-tuple-element.84, f32[]{:T(128)} %get-tuple-element.85), channel_id=1, replica_groups=mesh['tm'=2,'lat'=4,'lon'=4] {'lat'}, use_global_device_ids=true, to_apply=%region_29.30 | all-reduce | flops 2 | bytes 16 | tf_op jit(solution)/shard_map/psum | solution.py:71
  173.3 9.1 %all-reduce.10 = (f32[]{:T(128)}, f32[]{:T(128)}) all-reduce(f32[]{:T(128)} %get-tuple-element.53, f32[]{:T(128)} %get-tuple-element.52), channel_id=1, replica_groups=mesh['tm'=2,'lat'=4,'lon'=4] {'lon'}, use_global_device_ids=true, to_apply=%region_34.35 | all-reduce | flops 2 | bytes 16 | tf_op jit(solution)/shard_map/psum | solution.py:72
  204.6 9.1 %all-reduce.9 = (f32[]{:T(128)}, f32[]{:T(128)}) all-reduce(f32[]{:T(128)} %get-tuple-element.51, f32[]{:T(128)} %get-tuple-element.50), channel_id=1, replica_groups=mesh['tm'=2,'lat'=4,'lon'=4] {'lon'}, use_global_device_ids=true, to_apply=%region_40.41 | all-reduce | flops 2 | bytes 16 | tf_op jit(solution)/shard_map/psum | solution.py:72
  226.9 33.0 %all-reduce.1 = (f32[]{:T(128)}, f32[]{:T(128)}) all-reduce(f32[]{:T(128)} %get-tuple-element.47, f32[]{:T(128)} %get-tuple-element.21), channel_id=1, replica_groups=mesh['tm'=2,'lat'=4,'lon'=4] {'lat','lon'}, use_global_device_ids=true, to_apply=%region_1.2 | all-reduce | flops 2 | bytes 16 | tf_op jit(solution)/shard_map/while/body/eval_jaxpr/psum | solution.py:100
  262.7 9.1 %all-reduce.8 = (f32[]{:T(128)}, f32[]{:T(128)}) all-reduce(f32[]{:T(128)} %get-tuple-element.49, f32[]{:T(128)} %get-tuple-element.48), channel_id=1, replica_groups=mesh['tm'=2,'lat'=4,'lon'=4] {'lon'}, use_global_device_ids=true, to_apply=%region_46.47 | all-reduce | flops 2 | bytes 16 | tf_op jit(solution)/shard_map/psum | solution.py:72
  282.6 8.7 %collective-permute-done.36 = f32[128,512]{1,0:T(8,128)S(1)} collective-permute-done((f32[128,512]{1,0:T(8,128)S(1)}, f32[128,512]{1,0:T(8,128)S(1)}, u32[]{:S(2)}, u32[]{:S(2)}) %collective-permute-start.36) | collective-permute-done | bytes 262176 | tf_op jit(solution)/shard_map/while/body/eval_jaxpr/ppermute | solution.py:29
  303.7 30.4 %all-reduce = (f32[]{:T(128)}, f32[]{:T(128)}) all-reduce(f32[]{:T(128)} %get-tuple-element.25, f32[]{:T(128)} %get-tuple-element.23), channel_id=1, replica_groups=mesh['tm'=2,'lat'=4,'lon'=4] {'lat','lon'}, use_global_device_ids=true, to_apply=%region_52.53 | all-reduce | flops 2 | bytes 16 | tf_op jit(solution)/shard_map/psum | solution.py:100
  334.7 11.2 %all-reduce.7 = (f32[]{:T(128)}, f32[]{:T(128)}) all-reduce(f32[]{:T(128)} %get-tuple-element.25, f32[]{:T(128)} %get-tuple-element.24), channel_id=1, replica_groups=mesh['tm'=2,'lat'=4,'lon'=4] {'lon'}, use_global_device_ids=true, to_apply=%region_55.0 | all-reduce | flops 2 | bytes 16 | tf_op jit(solution)/shard_map/psum | solution.py:72
  345.9 6.4 %all-reduce.21 = (f32[]{:T(128)}, f32[]{:T(128)}) all-reduce(f32[]{:T(128)} %get-tuple-element.76, f32[]{:T(128)} %get-tuple-element.77), channel_id=1, replica_groups=mesh['tm'=2,'lat'=4,'lon'=4] {'lat'}, use_global_device_ids=true, to_apply=%region_56.0 | all-reduce | flops 2 | bytes 16 | tf_op jit(solution)/shard_map/psum | solution.py:71
  365.2 9.6 %all-reduce.6 = (f32[]{:T(128)}, f32[]{:T(128)}) all-reduce(f32[]{:T(128)} %get-tuple-element.46, f32[]{:T(128)} %get-tuple-element.45), channel_id=1, replica_groups=mesh['tm'=2,'lat'=4,'lon'=4] {'lon'}, use_global_device_ids=true, to_apply=%region_61.62 | all-reduce | flops 2 | bytes 16 | tf_op jit(solution)/shard_map/psum | solution.py:72
  374.8 6.3 %all-reduce.20 = (f32[]{:T(128)}, f32[]{:T(128)}) all-reduce(f32[]{:T(128)} %get-tuple-element.74, f32[]{:T(128)} %get-tuple-element.75), channel_id=1, replica_groups=mesh['tm'=2,'lat'=4,'lon'=4] {'lat'}, use_global_device_ids=true, to_apply=%region_62.63 | all-reduce | flops 2 | bytes 16 | tf_op jit(solution)/shard_map/psum | solution.py:71
  396.7 9.0 %all-reduce.5 = (f32[]{:T(128)}, f32[]{:T(128)}) all-reduce(f32[]{:T(128)} %get-tuple-element.44, f32[]{:T(128)} %get-tuple-element.43), channel_id=1, replica_groups=mesh['tm'=2,'lat'=4,'lon'=4] {'lon'}, use_global_device_ids=true, to_apply=%region_67.68 | all-reduce | flops 2 | bytes 16 | tf_op jit(solution)/shard_map/psum | solution.py:72
  405.7 6.3 %all-reduce.19 = (f32[]{:T(128)}, f32[]{:T(128)}) all-reduce(f32[]{:T(128)} %get-tuple-element.72, f32[]{:T(128)} %get-tuple-element.73), channel_id=1, replica_groups=mesh['tm'=2,'lat'=4,'lon'=4] {'lat'}, use_global_device_ids=true, to_apply=%region_68.69 | all-reduce | flops 2 | bytes 16 | tf_op jit(solution)/shard_map/psum | solution.py:71
  426.3 9.0 %all-reduce.4 = (f32[]{:T(128)}, f32[]{:T(128)}) all-reduce(f32[]{:T(128)} %get-tuple-element.42, f32[]{:T(128)} %get-tuple-element.41), channel_id=1, replica_groups=mesh['tm'=2,'lat'=4,'lon'=4] {'lon'}, use_global_device_ids=true, to_apply=%region_73.74 | all-reduce | flops 2 | bytes 16 | tf_op jit(solution)/shard_map/psum | solution.py:72
  457.7 9.0 %all-reduce.3 = (f32[]{:T(128)}, f32[]{:T(128)}) all-reduce(f32[]{:T(128)} %get-tuple-element.40, f32[]{:T(128)} %get-tuple-element.38), channel_id=1, replica_groups=mesh['tm'=2,'lat'=4,'lon'=4] {'lon'}, use_global_device_ids=true, to_apply=%region_79.80 | all-reduce | flops 2 | bytes 16 | tf_op jit(solution)/shard_map/psum | solution.py:72
  466.7 6.3 %all-reduce.17 = (f32[]{:T(128)}, f32[]{:T(128)}) all-reduce(f32[]{:T(128)} %get-tuple-element.68, f32[]{:T(128)} %get-tuple-element.69), channel_id=1, replica_groups=mesh['tm'=2,'lat'=4,'lon'=4] {'lat'}, use_global_device_ids=true, to_apply=%region_80.81 | all-reduce | flops 2 | bytes 16 | tf_op jit(solution)/shard_map/psum | solution.py:71
  487.2 9.0 %all-reduce.2 = (f32[]{:T(128)}, f32[]{:T(128)}) all-reduce(f32[]{:T(128)} %get-tuple-element.36, f32[]{:T(128)} %get-tuple-element.26), channel_id=1, replica_groups=mesh['tm'=2,'lat'=4,'lon'=4] {'lon'}, use_global_device_ids=true, to_apply=%region_85.86 | all-reduce | flops 2 | bytes 16 | tf_op jit(solution)/shard_map/psum | solution.py:72
  (201 shorter events, 220.4 us)
Async XLA Ops:
  0.7 10.6 %collective-permute-start.5 = (f32[1,512]{1,0:T(1,128)S(1)}, f32[1,512]{1,0:T(1,128)S(1)}, u32[]{:S(2)}, u32[]{:S(2)}) collective-permute-start(f32[1,512]{1,0:T(1,128)S(1)} %get-tuple-element.195), channel_id=1, source_target_pairs={{4,0},{8,4},{12,8},{0,12},{5,1},{9,5},{13,9},{1,13},{6,2},{10,6},{... | collective-permute-start | bytes 6152 | tf_op jit(solution)/shard_map/while/body/eval_jaxpr/ppermute | solution.py:21
  3.2 8.2 %collective-permute-start.4 = (f32[1,512]{1,0:T(1,128)S(1)}, f32[1,512]{1,0:T(1,128)S(1)}, u32[]{:S(2)}, u32[]{:S(2)}) collective-permute-start(f32[1,512]{1,0:T(1,128)S(1)} %get-tuple-element.196), channel_id=1, source_target_pairs={{0,4},{4,8},{8,12},{12,0},{1,5},{5,9},{9,13},{13,1},{2,6},{6,10},{... | collective-permute-start | bytes 6152 | tf_op jit(solution)/shard_map/while/body/eval_jaxpr/ppermute | solution.py:18
  7.5 8.3 %collective-permute-start.2 = (f32[2,130,1]{2,1,0:T(8,128)S(1)}, f32[2,130,1]{2,1,0:T(8,128)S(1)}, u32[]{:S(2)}, u32[]{:S(2)}) collective-permute-start(f32[2,130,1]{2,1,0:T(8,128)S(1)} %get-tuple-element.135), channel_id=1, source_target_pairs={{0,1},{1,2},{2,3},{3,0},{4,5},{5,6},{6,7},{7,4},{8,9},{9,10},{10,1... | collective-permute-start | bytes 3128 | tf_op jit(solution)/shard_map/ppermute | solution.py:18
  9.1 9.5 %collective-permute-start.3 = (f32[2,130,1]{2,1,0:T(8,128)S(1)}, f32[2,130,1]{2,1,0:T(8,128)S(1)}, u32[]{:S(2)}, u32[]{:S(2)}) collective-permute-start(f32[2,130,1]{2,1,0:T(8,128)S(1)} %get-tuple-element.136), channel_id=1, source_target_pairs={{1,0},{2,1},{3,2},{0,3},{5,4},{6,5},{7,6},{4,7},{9,8},{10,9},{11,1... | collective-permute-start | bytes 3128 | tf_op jit(solution)/shard_map/ppermute | solution.py:21
  11.5 8.5 %collective-permute-start.6 = (f32[130,1]{1,0:T(8,128)S(1)}, f32[130,1]{1,0:T(8,128)S(1)}, u32[]{:S(2)}, u32[]{:S(2)}) collective-permute-start(f32[130,1]{1,0:T(8,128)S(1)} %get-tuple-element.165), channel_id=1, source_target_pairs={{1,0},{2,1},{3,2},{0,3},{5,4},{6,5},{7,6},{4,7},{9,8},{10,9},{11,1... | collective-permute-start | bytes 1568 | tf_op jit(solution)/shard_map/while/body/eval_jaxpr/ppermute | solution.py:21
  13.3 8.4 %collective-permute-start.7 = (f32[130,1]{1,0:T(8,128)S(1)}, f32[130,1]{1,0:T(8,128)S(1)}, u32[]{:S(2)}, u32[]{:S(2)}) collective-permute-start(f32[130,1]{1,0:T(8,128)S(1)} %get-tuple-element.166), channel_id=1, source_target_pairs={{0,1},{1,2},{2,3},{3,0},{4,5},{5,6},{6,7},{7,4},{8,9},{9,10},{10,1... | collective-permute-start | bytes 1568 | tf_op jit(solution)/shard_map/while/body/eval_jaxpr/ppermute | solution.py:18
  44.8 5.1 %collective-permute-start.10 = (f32[130,1]{1,0:T(8,128)S(1)}, f32[130,1]{1,0:T(8,128)S(1)}, u32[]{:S(2)}, u32[]{:S(2)}) collective-permute-start(f32[130,1]{1,0:T(8,128)S(1)} %get-tuple-element.163), channel_id=1, source_target_pairs={{1,0},{2,1},{3,2},{0,3},{5,4},{6,5},{7,6},{4,7},{9,8},{10,9},{11,1... | collective-permute-start | bytes 1568 | tf_op jit(solution)/shard_map/ppermute | solution.py:21
  45.0 6.1 %collective-permute-start.11 = (f32[130,1]{1,0:T(8,128)S(1)}, f32[130,1]{1,0:T(8,128)S(1)}, u32[]{:S(2)}, u32[]{:S(2)}) collective-permute-start(f32[130,1]{1,0:T(8,128)S(1)} %get-tuple-element.164), channel_id=1, source_target_pairs={{0,1},{1,2},{2,3},{3,0},{4,5},{5,6},{6,7},{7,4},{8,9},{9,10},{10,1... | collective-permute-start | bytes 1568 | tf_op jit(solution)/shard_map/ppermute | solution.py:18
  76.3 6.1 %collective-permute-start.15 = (f32[130,1]{1,0:T(8,128)S(1)}, f32[130,1]{1,0:T(8,128)S(1)}, u32[]{:S(2)}, u32[]{:S(2)}) collective-permute-start(f32[130,1]{1,0:T(8,128)S(1)} %get-tuple-element.162), channel_id=1, source_target_pairs={{0,1},{1,2},{2,3},{3,0},{4,5},{5,6},{6,7},{7,4},{8,9},{9,10},{10,1... | collective-permute-start | bytes 1568 | tf_op jit(solution)/shard_map/ppermute | solution.py:18
  105.6 6.1 %collective-permute-start.19 = (f32[130,1]{1,0:T(8,128)S(1)}, f32[130,1]{1,0:T(8,128)S(1)}, u32[]{:S(2)}, u32[]{:S(2)}) collective-permute-start(f32[130,1]{1,0:T(8,128)S(1)} %get-tuple-element.160), channel_id=1, source_target_pairs={{0,1},{1,2},{2,3},{3,0},{4,5},{5,6},{6,7},{7,4},{8,9},{9,10},{10,1... | collective-permute-start | bytes 1568 | tf_op jit(solution)/shard_map/ppermute | solution.py:18
  136.9 6.1 %collective-permute-start.23 = (f32[130,1]{1,0:T(8,128)S(1)}, f32[130,1]{1,0:T(8,128)S(1)}, u32[]{:S(2)}, u32[]{:S(2)}) collective-permute-start(f32[130,1]{1,0:T(8,128)S(1)} %get-tuple-element.158), channel_id=1, source_target_pairs={{0,1},{1,2},{2,3},{3,0},{4,5},{5,6},{6,7},{7,4},{8,9},{9,10},{10,1... | collective-permute-start | bytes 1568 | tf_op jit(solution)/shard_map/ppermute | solution.py:18
  166.2 6.1 %collective-permute-start.27 = (f32[130,1]{1,0:T(8,128)S(1)}, f32[130,1]{1,0:T(8,128)S(1)}, u32[]{:S(2)}, u32[]{:S(2)}) collective-permute-start(f32[130,1]{1,0:T(8,128)S(1)} %get-tuple-element.156), channel_id=1, source_target_pairs={{0,1},{1,2},{2,3},{3,0},{4,5},{5,6},{6,7},{7,4},{8,9},{9,10},{10,1... | collective-permute-start | bytes 1568 | tf_op jit(solution)/shard_map/ppermute | solution.py:18
  197.5 6.1 %collective-permute-start.31 = (f32[130,1]{1,0:T(8,128)S(1)}, f32[130,1]{1,0:T(8,128)S(1)}, u32[]{:S(2)}, u32[]{:S(2)}) collective-permute-start(f32[130,1]{1,0:T(8,128)S(1)} %get-tuple-element.154), channel_id=1, source_target_pairs={{0,1},{1,2},{2,3},{3,0},{4,5},{5,6},{6,7},{7,4},{8,9},{9,10},{10,1... | collective-permute-start | bytes 1568 | tf_op jit(solution)/shard_map/ppermute | solution.py:18
  224.8 36.9 %collective-permute-start.34 = (f32[130,1]{1,0:T(8,128)S(1)}, f32[130,1]{1,0:T(8,128)S(1)}, u32[]{:S(2)}, u32[]{:S(2)}) collective-permute-start(f32[130,1]{1,0:T(8,128)S(1)} %get-tuple-element.151), channel_id=1, source_target_pairs={{1,0},{2,1},{3,2},{0,3},{5,4},{6,5},{7,6},{4,7},{9,8},{10,9},{11,1... | collective-permute-start | bytes 1568 | tf_op jit(solution)/shard_map/ppermute | solution.py:21
  226.8 34.9 %collective-permute-start.35 = (f32[130,1]{1,0:T(8,128)S(1)}, f32[130,1]{1,0:T(8,128)S(1)}, u32[]{:S(2)}, u32[]{:S(2)}) collective-permute-start(f32[130,1]{1,0:T(8,128)S(1)} %get-tuple-element.152), channel_id=1, source_target_pairs={{0,1},{1,2},{2,3},{3,0},{4,5},{5,6},{6,7},{7,4},{8,9},{9,10},{10,1... | collective-permute-start | bytes 1568 | tf_op jit(solution)/shard_map/ppermute | solution.py:18
  281.3 10.0 %collective-permute-start.36 = (f32[128,512]{1,0:T(8,128)S(1)}, f32[128,512]{1,0:T(8,128)S(1)}, u32[]{:S(2)}, u32[]{:S(2)}) collective-permute-start(f32[128,512]{1,0:T(8,128)S(1)} %get-tuple-element.125), channel_id=1, source_target_pairs={{16,0},{17,1},{18,2},{19,3},{20,4},{21,5},{22,6},{23,7},{24,8},{25... | collective-permute-start | bytes 786440 | tf_op jit(solution)/shard_map/while/body/eval_jaxpr/ppermute | solution.py:29
  294.5 4.4 collective-permute-start.39
  296.6 6.1 %collective-permute-start.40 = (f32[130,1]{1,0:T(8,128)S(1)}, f32[130,1]{1,0:T(8,128)S(1)}, u32[]{:S(2)}, u32[]{:S(2)}) collective-permute-start(f32[130,1]{1,0:T(8,128)S(1)} %get-tuple-element.150), channel_id=1, source_target_pairs={{0,1},{1,2},{2,3},{3,0},{4,5},{5,6},{6,7},{7,4},{8,9},{9,10},{10,1... | collective-permute-start | bytes 1568 | tf_op jit(solution)/shard_map/ppermute | solution.py:18
  358.0 5.1 %collective-permute-start.43 = (f32[130,1]{1,0:T(8,128)S(1)}, f32[130,1]{1,0:T(8,128)S(1)}, u32[]{:S(2)}, u32[]{:S(2)}) collective-permute-start(f32[130,1]{1,0:T(8,128)S(1)} %get-tuple-element.147), channel_id=1, source_target_pairs={{1,0},{2,1},{3,2},{0,3},{5,4},{6,5},{7,6},{4,7},{9,8},{10,9},{11,1... | collective-permute-start | bytes 1568 | tf_op jit(solution)/shard_map/ppermute | solution.py:21
  358.1 6.2 %collective-permute-start.44 = (f32[130,1]{1,0:T(8,128)S(1)}, f32[130,1]{1,0:T(8,128)S(1)}, u32[]{:S(2)}, u32[]{:S(2)}) collective-permute-start(f32[130,1]{1,0:T(8,128)S(1)} %get-tuple-element.148), channel_id=1, source_target_pairs={{0,1},{1,2},{2,3},{3,0},{4,5},{5,6},{6,7},{7,4},{8,9},{9,10},{10,1... | collective-permute-start | bytes 1568 | tf_op jit(solution)/shard_map/ppermute | solution.py:18
  389.6 6.1 %collective-permute-start.48 = (f32[130,1]{1,0:T(8,128)S(1)}, f32[130,1]{1,0:T(8,128)S(1)}, u32[]{:S(2)}, u32[]{:S(2)}) collective-permute-start(f32[130,1]{1,0:T(8,128)S(1)} %get-tuple-element.146), channel_id=1, source_target_pairs={{0,1},{1,2},{2,3},{3,0},{4,5},{5,6},{6,7},{7,4},{8,9},{9,10},{10,1... | collective-permute-start | bytes 1568 | tf_op jit(solution)/shard_map/ppermute | solution.py:18
  419.2 6.1 %collective-permute-start.52 = (f32[130,1]{1,0:T(8,128)S(1)}, f32[130,1]{1,0:T(8,128)S(1)}, u32[]{:S(2)}, u32[]{:S(2)}) collective-permute-start(f32[130,1]{1,0:T(8,128)S(1)} %get-tuple-element.144), channel_id=1, source_target_pairs={{0,1},{1,2},{2,3},{3,0},{4,5},{5,6},{6,7},{7,4},{8,9},{9,10},{10,1... | collective-permute-start | bytes 1568 | tf_op jit(solution)/shard_map/ppermute | solution.py:18
  450.6 6.1 %collective-permute-start.56 = (f32[130,1]{1,0:T(8,128)S(1)}, f32[130,1]{1,0:T(8,128)S(1)}, u32[]{:S(2)}, u32[]{:S(2)}) collective-permute-start(f32[130,1]{1,0:T(8,128)S(1)} %get-tuple-element.142), channel_id=1, source_target_pairs={{0,1},{1,2},{2,3},{3,0},{4,5},{5,6},{6,7},{7,4},{8,9},{9,10},{10,1... | collective-permute-start | bytes 1568 | tf_op jit(solution)/shard_map/ppermute | solution.py:18
  480.2 6.1 %collective-permute-start.60 = (f32[130,1]{1,0:T(8,128)S(1)}, f32[130,1]{1,0:T(8,128)S(1)}, u32[]{:S(2)}, u32[]{:S(2)}) collective-permute-start(f32[130,1]{1,0:T(8,128)S(1)} %get-tuple-element.140), channel_id=1, source_target_pairs={{0,1},{1,2},{2,3},{3,0},{4,5},{5,6},{6,7},{7,4},{8,9},{9,10},{10,1... | collective-permute-start | bytes 1568 | tf_op jit(solution)/shard_map/ppermute | solution.py:18
  (40 other events, 143.9 us)
